TPU v7x, 8 devices: a whole 2x2x1 slice. The times are simulated.
8 devices in a mesh: rep: 1 (over z), dp: 8 (over x, y, core).
Axes of the slice: x: 2, y: 2, z: 1, core: 2. Of those that a mesh axis runs over, the one named last changes fastest.
Arguments:
- x: bfloat16 [8, 2048, 1024], P(('rep', 'dp'))
- dy: bfloat16 [8, 2048, 1024], P(('rep', 'dp'))
- w_gate: bfloat16 [2, 1024, 3200], replicated
- w_up: bfloat16 [2, 1024, 3200], replicated
- w_down: bfloat16 [2, 3200, 1024], replicated
- m_w_gate: float32 [2, 1024, 3200], replicated
- m_w_up: float32 [2, 1024, 3200], replicated
- m_w_down: float32 [2, 3200, 1024], replicated
- v_w_gate: float32 [2, 1024, 3200], replicated
- v_w_up: float32 [2, 1024, 3200], replicated
- v_w_down: float32 [2, 3200, 1024], replicated
Outputs:
- output 1: bfloat16 [2, 1024, 3200], P('rep')
- output 2: bfloat16 [2, 1024, 3200], P('rep')
- output 3: bfloat16 [2, 3200, 1024], P('rep')
- output 4: float32 [2, 1024, 3200], P('rep')
- output 5: float32 [2, 1024, 3200], P('rep')
- output 6: float32 [2, 3200, 1024], P('rep')
- output 7: float32 [2, 1024, 3200], P('rep')
- output 8: float32 [2, 1024, 3200], P('rep')
- output 9: float32 [2, 3200, 1024], P('rep')
All inputs are finite; a program needn't handle non-finite values.
Results may differ from a plain program's by a relative error of at most 0.0225.
Values are sent between devices in bfloat16 or wider.
A program may use at most 2.75 GiB of HBM per device.

v0:
```python
import jax
import jax.numpy as jnp
from jax import lax
from jax.sharding import PartitionSpec as P

NAMES = ("w_gate", "w_up", "w_down")


def matmul(a, w):
    return jnp.dot(a, w, preferred_element_type=jnp.float32).astype(jnp.bfloat16)


def normed(h):
    wide = h.astype(jnp.float32)
    scale = lax.rsqrt(jnp.mean(wide**2, -1, keepdims=True) + 1e-6)
    return (wide * scale).astype(jnp.bfloat16)


def layer(h, w):
    a = normed(h)
    gate = jnp.dot(a, w["w_gate"], preferred_element_type=jnp.float32)
    up = jnp.dot(a, w["w_up"], preferred_element_type=jnp.float32)
    return h + matmul((jax.nn.silu(gate) * up).astype(jnp.bfloat16), w["w_down"])


def adamw(w, m, v, g):
    m = 0.9 * m + 0.1 * g
    v = 0.95 * v + 0.05 * g * g
    step = m * lax.rsqrt(v + 1e-8) + 0.1 * w
    return (w - 0.02 * step).astype(jnp.bfloat16), m, v


def solution(mesh):
    def step(x, dy, *arrays):
        weights, m, v = (arrays[i : i + 3] for i in (0, 3, 6))
        layers = weights[0].shape[0]
        h, kept = x[0], []
        for number in range(layers):
            kept.append(h)
            h = layer(h, {name: w[number] for name, w in zip(NAMES, weights, strict=True)})
        by_h, summed = dy[0], [None] * layers
        for number in reversed(range(layers)):
            _, back = jax.vjp(lambda w, h: layer(h, w), {name: w[number] for name, w in zip(NAMES, weights, strict=True)}, kept[number])
            by_w, by_h = back(by_h)
            summed[number] = [lax.psum(by_w[name], "dp") for name in NAMES]
        gradients = [jnp.stack([summed[number][i] for number in range(layers)]).astype(jnp.float32) for i in range(3)]
        new = [adamw(w.astype(jnp.float32), m, v, g) for w, m, v, g in zip(weights, m, v, gradients, strict=True)]
        return tuple(one[which] for which in range(3) for one in new)

    return jax.shard_map(
        step,
        mesh=mesh,
        in_specs=(P(("rep", "dp"), None, None),) * 2 + (P(None, None, None),) * 9,
        out_specs=(P("rep", None, None),) * 9,
        check_vma=False,
    )
```

profile of v0, /device:TPU:0, one launch (start us, length us, event | category | flops | bytes accessed | tf_op | source)
XLA Modules:
  0.0 999.6 jit_solution(10259402501255425564)
XLA Ops:
  7.2 0.0 all-reduce.3.cloned.1.call-start
  7.2 6.5 copy.20
  13.7 3.1 fusion.30
  16.8 6.5 copy.21
  23.3 20.9 %convolution_convert_fusion.1 = bf16[2048,3200]{1,0:T(8,128)(2,1)} fusion(bf16[2,3200,1024]{2,1,0:T(8,128)(2,1)} %param.15, bf16[1,2048,1024]{2,1,0:T(8,128)(2,1)} %param.12), kind=kOutput, calls=%fused_computation.50 | convolution fusion | flops 13428326400 | bytes 23855104 | tf_op jit(solution)/shard_map/transpose(jvp())/dot_general | solution.py:10
  44.2 21.0 %fusion.56 = f32[2048,3200]{1,0:T(8,128)} fusion(bf16[2,1024,3200]{2,1,0:T(8,128)(2,1)} %param.13, bf16[1,2048,1024]{2,1,0:T(8,128)(2,1)S(1)} %copy-done.3, f32[2048]{0:T(1024)S(1)} %add_rsqrt_fusion), kind=kOutput, calls=%fused_computation.90 | convolution fusion | flops 13428064256 | bytes 36970496 | tf_op jit(solution)/shard_map/dot_general | solution.py:21
  65.2 32.2 %multiply_convert_fusion.1 = (bf16[2048,3200]{1,0:T(8,128)(2,1)}, f32[2048,3200]{1,0:T(8,128)}) fusion(f32[2048,3200]{1,0:T(8,128)} %fusion.56, bf16[2,1024,3200]{2,1,0:T(8,128)(2,1)} %param.14, bf16[1,2048,1024]{2,1,0:T(8,128)(2,1)} %param.11, f32[2048]{0:T(1024)S(1)} %add_rsqrt_fusion), kind=kOutput, calls=%fused_computation.44 | convolution fusion | flops 13467385856 | bytes 76292096 | tf_op jit(solution)/shard_map/dot_general | solution.py:22
  97.4 21.9 %fusion.34 = (f32[2048]{0:T(1024)S(1)}, bf16[2048,1024]{0,1:T(8,128)(2,1)}) fusion(bf16[2048,3200]{1,0:T(8,128)(2,1)} %get-tuple-element.24, bf16[2,3200,1024]{2,1,0:T(8,128)(2,1)} %param.15, bf16[1,2048,1024]{1,2,0:T(8,128)(2,1)} %copy.20), kind=kOutput, calls=%fused_computation.67 | convolution fusion | flops 13432256512 | bytes 28057600 | tf_op jit(solution)/shard_map/dot_general | solution.py:10
  119.3 23.3 %fusion.43 = f32[2048,3200]{1,0:T(8,128)} fusion(bf16[2,1024,3200]{2,1,0:T(8,128)(2,1)} %param.14, bf16[2048,1024]{0,1:T(8,128)(2,1)} %get-tuple-element.27, f32[2048]{0:T(1024)S(1)} %fusion.92), kind=kOutput, calls=%fused_computation.77 | convolution fusion | flops 13428064256 | bytes 36970496 | tf_op jit(solution)/shard_map/jvp()/dot_general | solution.py:22
  142.6 38.9 %fusion.14 = (bf16[2048,3200]{1,0:T(8,128)(2,1)}, f32[2048,3200]{1,0:T(8,128)}) fusion(f32[2048,3200]{1,0:T(8,128)} %fusion.43, bf16[2048,3200]{1,0:T(8,128)(2,1)} %convolution_convert_fusion.1, bf16[2,1024,3200]{2,1,0:T(8,128)(2,1)} %param.13, bf16[2048,1024]{0,1:T(8,128)(2,1)} %get-tuple-element.27, f32[2048]{0:T(1024)S(1)} %fusion.92), kind=kOutput, calls=%fused_computation.32 | convolution fusion | flops 13506707456 | bytes 89399296 | tf_op jit(solution)/shard_map/jvp()/dot_general | solution.py:21
  181.6 22.6 %fusion.27 = bf16[2048,1024]{0,1:T(8,128)(2,1)} fusion(bf16[2048,3200]{1,0:T(8,128)(2,1)} %convolution_convert_fusion.1, bf16[2,1024,3200]{2,1,0:T(8,128)(2,1)} %param.14, f32[2048,3200]{1,0:T(8,128)} %get-tuple-element.29), kind=kOutput, calls=%fused_computation.48 | convolution fusion | flops 13461094400 | bytes 50069504 | tf_op jit(solution)/shard_map/transpose(jvp())/dot_general | solution.py:22
  204.2 24.2 %fusion.64 = bf16[1,1024,3200]{2,1,0:T(8,128)(2,1)} fusion(bf16[2048,3200]{1,0:T(8,128)(2,1)} %convolution_convert_fusion.1, bf16[2048,1024]{0,1:T(8,128)(2,1)S(1)} %copy-done.2, f32[2048]{0:T(1024)S(1)} %fusion.92, f32[2048,3200]{1,0:T(8,128)} %get-tuple-element.29), kind=kOutput, calls=%fused_computation.98 | convolution fusion | flops 13470662656 | bytes 50077696 | tf_op jit(solution)/shard_map/transpose(jvp())/dot_general | solution.py:22
  228.4 25.7 %fusion.65 = bf16[1,3200,1024]{2,1,0:T(8,128)(2,1)} fusion(f32[2048,3200]{1,0:T(8,128)} %fusion.43, bf16[1,2048,1024]{2,1,0:T(8,128)(2,1)} %param.12, f32[2048,3200]{1,0:T(8,128)} %get-tuple-element.29), kind=kOutput, calls=%fused_computation.99 | convolution fusion | flops 13464371200 | bytes 63176704 | tf_op jit(solution)/shard_map/transpose(jvp())/dot_general | solution.py:10
  254.0 21.2 %fusion.61 = bf16[1,1024,3200]{2,1,0:T(8,128)(2,1)} fusion(bf16[2048,3200]{1,0:T(8,128)(2,1)} %get-tuple-element.28, bf16[2048,1024]{0,1:T(8,128)(2,1)} %get-tuple-element.27, f32[2048]{0:T(1024)S(1)} %fusion.92), kind=kOutput, calls=%fused_computation.95 | convolution fusion | flops 13428064256 | bytes 23863296 | tf_op jit(solution)/shard_map/transpose(jvp())/dot_general | solution.py:21
  275.3 22.8 %fusion.36 = (f32[2048]{0:T(1024)S(1)}, bf16[2048,1024]{0,1:T(8,128)(2,1)}) fusion(bf16[2048,1024]{0,1:T(8,128)(2,1)} %get-tuple-element.27, bf16[2048,1024]{0,1:T(8,128)(2,1)} %fusion.27, bf16[2048,3200]{1,0:T(8,128)(2,1)} %get-tuple-element.28, bf16[2,1024,3200]{2,1,0:T(8,128)(2,1)} %param.13), kind=kOutput, calls=%fused_computation.69 | convolution fusion | flops 13432256512 | bytes 32251904 | tf_op jit(solution)/shard_map/transpose(jvp())/dot_general | solution.py:21
  298.1 6.6 fusion.77
  304.7 21.1 %convolution_convert_fusion = bf16[2048,3200]{1,0:T(8,128)(2,1)} fusion(bf16[2048,1024]{0,1:T(8,128)(2,1)} %fusion.77, bf16[2,3200,1024]{2,1,0:T(8,128)(2,1)} %param.15), kind=kOutput, calls=%fused_computation.49 | convolution fusion | flops 13428326400 | bytes 23855104 | tf_op jit(solution)/shard_map/transpose(jvp())/dot_general | solution.py:10
  325.8 21.2 %fusion.62 = bf16[1,3200,1024]{2,1,0:T(8,128)(2,1)} fusion(bf16[2048,3200]{1,0:T(8,128)(2,1)} %get-tuple-element.24, bf16[2048,1024]{0,1:T(8,128)(2,1)} %fusion.77), kind=kOutput, calls=%fused_computation.96 | convolution fusion | flops 13425049600 | bytes 23855104 | tf_op jit(solution)/shard_map/transpose(jvp())/dot_general | solution.py:10
  347.0 24.2 %fusion.63 = bf16[1,1024,3200]{2,1,0:T(8,128)(2,1)} fusion(bf16[2048,3200]{1,0:T(8,128)(2,1)} %convolution_convert_fusion, f32[2048,3200]{1,0:T(8,128)} %fusion.56, bf16[1,2048,1024]{1,2,0:T(8,128)(2,1)S(1)} %copy-done.1, f32[2048]{0:T(1024)S(1)} %copy-done.7), kind=kOutput, calls=%fused_computation.97 | convolution fusion | flops 13470662656 | bytes 50077696 | tf_op jit(solution)/shard_map/transpose(jvp())/dot_general | solution.py:22
  371.2 29.7 %fusion.66 = bf16[1,1024,3200]{2,1,0:T(8,128)(2,1)} fusion(f32[2048,3200]{1,0:T(8,128)} %fusion.56, f32[2048,3200]{1,0:T(8,128)} %get-tuple-element.25, bf16[2048,3200]{1,0:T(8,128)(2,1)} %convolution_convert_fusion, bf16[1,2048,1024]{1,2,0:T(8,128)(2,1)S(1)} %copy-done.1, f32[2048]{0:T(1024)S(1)} %copy-done.7), kind=kOutput, calls=%fused_computation.100 | convolution fusion | flops 13503430656 | bytes 76292096 | tf_op jit(solution)/shard_map/transpose(jvp())/dot_general | solution.py:21
  400.9 0.0 all-reduce.3.cloned.1.call-update
  400.9 450.3 %all-reduce.3.cloned.1.call-done = (bf16[1,1024,3200]{2,1,0:T(8,128)(2,1)}, bf16[1,1024,3200]{2,1,0:T(8,128)(2,1)}, bf16[1,1024,3200]{2,1,0:T(8,128)(2,1)}, bf16...) async-done(((bf16[1,1024,3200]{2,1,0:T(8,128)(2,1)}, bf16[1,1024,3200]{2,1,0:T(8,128)(2,1)}, ...) | async-done | bytes 39321616 | tf_op jit(solution)/shard_map/psum | solution.py:45
  851.2 49.7 %fusion.11 = (bf16[2,3200,1024]{2,1,0:T(8,128)(2,1)}, f32[2,3200,1024]{2,1,0:T(8,128)}, f32[2,3200,1024]{2,1,0:T(8,128)}) fusion(bf16[2,3200,1024]{2,1,0:T(8,128)(2,1)} %param.15, bf16[1,3200,1024]{2,1,0:T(8,128)(2,1)} %get-tuple-element.13, bf16[1,3200,1024]{2,1,0:T(8,128)(2,1)} %get-tuple-element.14, f32[2,3200,1024]{2,1,0:T(8,128)} %param.21, ...), kind=kLoop, calls=%fused_computation.29 | loop fusion | flops 124518400 | bytes 144179200 | tf_op jit(solution)/shard_map/convert_element_type | solution.py:30
  900.9 91.6 %fusion.2 = (bf16[2,1024,3200]{2,1,0:T(8,128)(2,1)}, f32[2,1024,3200]{2,1,0:T(8,128)}, f32[2,1024,3200]{2,1,0:T(8,128)}, bf16[2,1024,3200]{2,1,0:T(8,128)(2,1)},...) fusion(bf16[2,1024,3200]{2,1,0:T(8,128)(2,1)} %param.13, bf16[1,1024,3200]{2,1,0:T(8,128)(2,1)} %get-tuple-element.9, ...), kind=kLoop, calls=%fused_computation.20 | loop fusion | flops 249036800 | bytes 288358400 | tf_op jit(solution)/shard_map/convert_element_type | solution.py:30
  (19 shorter events, 0.1 us)
Async XLA Ops:
  7.2 844.0 %all-reduce.3.cloned.1.call-start = ((), (), s32[]{:S(2)}) async-start(), calls=%async_computation | async-start | bytes 78643200 | tf_op jit(solution)/shard_map/psum | solution.py:45
  16.8 48.4 %copy-start.6 = (f32[2048]{0:T(1024)}, f32[2048]{0:T(1024)S(1)}, u32[]{:S(2)}) copy-start(f32[2048]{0:T(1024)S(1)} %add_rsqrt_fusion) | copy-start | bytes 24580
  23.3 20.9 %copy-start.3 = (bf16[1,2048,1024]{2,1,0:T(8,128)(2,1)S(1)}, bf16[1,2048,1024]{2,1,0:T(8,128)(2,1)}, u32[]{:S(2)}) copy-start(bf16[1,2048,1024]{2,1,0:T(8,128)(2,1)} %param.11) | copy-start | bytes 12582916
  119.3 23.3 %copy-start.4 = (f32[2048]{0:T(1024)}, f32[2048]{0:T(1024)S(1)}, u32[]{:S(2)}) copy-start(f32[2048]{0:T(1024)S(1)} %get-tuple-element.26) | copy-start | bytes 24580
  181.5 22.6 %copy-start.2 = (bf16[2048,1024]{0,1:T(8,128)(2,1)S(1)}, bf16[2048,1024]{0,1:T(8,128)(2,1)}, u32[]{:S(2)}) copy-start(bf16[2048,1024]{0,1:T(8,128)(2,1)} %get-tuple-element.27) | copy-start | bytes 12582916
  275.3 22.8 %copy-start.5 = (f32[2048]{0:T(1024)S(1)}, f32[2048]{0:T(1024)}, u32[]{:S(2)}) copy-start(f32[2048]{0:T(1024)} %copy-done.4) | copy-start | bytes 24580
  275.3 22.8 %copy-start = (bf16[1,2048,1024]{1,2,0:T(8,128)(2,1)S(1)}, bf16[1,2048,1024]{1,2,0:T(8,128)(2,1)}, u32[]{:S(2)}) copy-start(bf16[1,2048,1024]{1,2,0:T(8,128)(2,1)} %copy.21) | copy-start | bytes 12582916
  325.8 21.2 %copy-start.1 = (bf16[1,2048,1024]{1,2,0:T(8,128)(2,1)S(1)}, bf16[1,2048,1024]{1,2,0:T(8,128)(2,1)}, u32[]{:S(2)}) copy-start(bf16[1,2048,1024]{1,2,0:T(8,128)(2,1)} %copy.20) | copy-start | bytes 12582916
  325.8 21.2 %copy-start.7 = (f32[2048]{0:T(1024)S(1)}, f32[2048]{0:T(1024)}, u32[]{:S(2)}) copy-start(f32[2048]{0:T(1024)} %copy-done.6) | copy-start | bytes 24580
Sparse Core Ops, SparseCore 0:
  401.0 450.1 all-reduce.2
where the time goes:
time: 1010 us; the launch traced here: 1000 us
  waiting for transfers between devices  450 us (45%)
  matrix products  371 us (37%)
  other arithmetic  151 us (15%)
  between operations  14.3 us (1%)
  local copies, waits for them, and re-layouts  13 us (1%)
    psum x1, waiting for transfers between devices, step(): summed[number] = [lax.psum(by_w[name], 'dp') for name in NAMES]  450 us
    convert_element_type x2, other arithmetic, adamw(): return ((w - 0.02 * step).astype(jnp.bfloat16), m, v)  141 us
    dot_general x5, matrix products, layer(): gate = jnp.dot(a, w['w_gate'], preferred_element_type=jnp.float32)  134 us
    dot_general x5, matrix products, layer(): up = jnp.dot(a, w['w_up'], preferred_element_type=jnp.float32)  127 us
    dot_general x5, matrix products, matmul(): jnp.dot(a, w, preferred_element_type=jnp.float32).astype(jnp.bfloat16)  111 us
  transfers between devices with their start and end apart: 1, of which 1 were waited for; matrix products, arithmetic and copies ran while one was open for 0% of the time, Pallas kernels for 0%

commit v1 on v0

v1 whole, which is shorter than its diff:
```python
import functools

import jax
import jax.numpy as jnp
from jax import lax
from jax.experimental import pallas as pl
from jax.experimental.pallas import tpu as pltpu
from jax.sharding import PartitionSpec as P

NAMES = ("w_gate", "w_up", "w_down")
TOKENS, D, FF = 2048, 1024, 3200
BLOCK = 256
ROWS = 512
CHUNK = D // 8
VMEM = 66_000_000
NT = (((1,), (1,)), ((), ()))
F32, BF16 = jnp.float32, jnp.bfloat16


def dot(a, b):
    return jnp.dot(a, b, preferred_element_type=F32)


def dot_nt(a, b):
    return lax.dot_general(a, b, NT, preferred_element_type=F32)


def once(shape, index_map):
    return pl.BlockSpec(shape, index_map, pipeline_mode=pl.Buffered(1))


def rms(h):
    return lax.rsqrt(jnp.mean(h * h, -1, keepdims=True) + 1e-6)


def by_width(j, units, last, body):
    if last == BLOCK:
        pl.when(j < units)(lambda: body(BLOCK))
    else:
        pl.when(j < units - 1)(lambda: body(BLOCK))
        pl.when(j == units - 1)(lambda: body(last))


def forward_kernel(units, last, x_ref, wg_ref, wu_ref, wd_ref, gate_ref, up_ref, a_ref, h_ref, next_ref, acc):
    j = pl.program_id(0)

    @pl.when(j == 0)
    def _():
        @pl.loop(0, TOKENS // ROWS)
        def _(i):
            rows = pl.ds(pl.multiple_of(i * ROWS, ROWS), ROWS)
            wide = x_ref[rows, :].astype(F32)
            a_ref[rows, :] = (wide * rms(wide)).astype(BF16)
            acc[rows, :] = jnp.zeros((ROWS, D), F32)

    def body(width):
        @pl.loop(0, TOKENS // ROWS)
        def _(i):
            rows = pl.ds(pl.multiple_of(i * ROWS, ROWS), ROWS)
            a = a_ref[rows, :]
            gate = dot(a, wg_ref[:, :width])
            up = dot(a, wu_ref[:, :width])
            gate_ref[rows, :width] = gate
            up_ref[rows, :width] = up
            act = (gate * jax.nn.sigmoid(gate) * up).astype(BF16)
            acc[rows, :] += dot(act, wd_ref[:width, :])

    by_width(j, units, last, body)

    @pl.when(j == units - 1)
    def _():
        @pl.loop(0, TOKENS // ROWS)
        def _(i):
            rows = pl.ds(pl.multiple_of(i * ROWS, ROWS), ROWS)
            h = (x_ref[rows, :].astype(F32) + acc[rows, :].astype(BF16).astype(F32)).astype(BF16)
            h_ref[rows, :] = h
            wide = h.astype(F32)
            next_ref[rows, :] = (wide * rms(wide)).astype(BF16)


def forward(x, wg, wu, wd):
    units = pl.cdiv(FF, BLOCK)
    last = FF - (units - 1) * BLOCK
    whole = lambda j: (0, 0)
    return pl.pallas_call(
        functools.partial(forward_kernel, units, last),
        grid=(units,),
        in_specs=[
            once((TOKENS, D), whole),
            pl.BlockSpec((None, D, BLOCK), lambda j: (0, 0, j)),
            pl.BlockSpec((None, D, BLOCK), lambda j: (0, 0, j)),
            pl.BlockSpec((None, BLOCK, D), lambda j: (0, j, 0)),
        ],
        out_specs=[
            pl.BlockSpec((TOKENS, BLOCK), lambda j: (0, j)),
            pl.BlockSpec((TOKENS, BLOCK), lambda j: (0, j)),
            once((TOKENS, D), whole),
            once((TOKENS, D), whole),
            once((TOKENS, D), whole),
        ],
        out_shape=[jax.ShapeDtypeStruct((TOKENS, FF), F32)] * 2 + [jax.ShapeDtypeStruct((TOKENS, D), BF16)] * 3,
        scratch_shapes=[pltpu.VMEM((TOKENS, D), F32)],
        compiler_params=pltpu.CompilerParams(vmem_limit_bytes=VMEM),
        cost_estimate=pl.CostEstimate(flops=6 * TOKENS * D * FF, bytes_accessed=90_000_000, transcendentals=TOKENS * FF),
        name="forward0",
    )(x, wg, wu, wd)


def backward_kernel(units, last, inner, *refs):
    if inner:
        a_ref, dy_ref, wd_ref, gate_ref, up_ref, out_ref = refs[:6]
        rest = refs[6:]
    else:
        a_ref, dy_ref, wd_ref, wg_ref, wu_ref, out_ref, da_ref = refs[:7]
        rest = refs[7:]
    at, dyt, act_s, dg_s, du_s, stay, go, first, second, r_core, r_first, r_second = rest[:12]
    sems = rest[12:18]
    acc = None if inner else rest[18]
    core_send, core_recv, first_send, first_recv, second_send, second_recv = sems
    j = pl.program_id(0)
    me = lax.axis_index("dp")
    core, y, x = me % 2, (me // 2) % 2, me // 4
    partner = me + 1 - 2 * core
    along_x, along_y = me + 4 - 8 * x, me + 2 - 4 * y
    one = (1 - core) * along_x + core * along_y
    two = (1 - core) * along_y + core * along_x

    def copy_core(k):
        return pltpu.make_async_remote_copy(
            go.at[k % 2], r_core.at[k % 4], core_send.at[k], core_recv.at[k], device_id={"dp": partner}, device_id_type=pl.DeviceIdType.MESH
        )

    def copy_first(k):
        return pltpu.make_async_remote_copy(
            first.at[k % 2], r_first.at[k % 4], first_send.at[k], first_recv.at[k], device_id={"dp": one}, device_id_type=pl.DeviceIdType.MESH
        )

    def copy_second(k):
        return pltpu.make_async_remote_copy(
            second.at[k % 2], r_second.at[k % 4], second_send.at[k], second_recv.at[k], device_id={"dp": two}, device_id_type=pl.DeviceIdType.MESH
        )

    @pl.when(j == 0)
    def _():
        barrier = pltpu.get_barrier_semaphore()
        for other in (partner, along_x, along_y):
            pl.semaphore_signal(barrier, inc=1, device_id={"dp": other}, device_id_type=pl.DeviceIdType.MESH)
        pl.semaphore_wait(barrier, 3)
        for r in range(8):
            c, u, v = r // 4, (r // 2) % 2, r % 2
            owner_core = (core + c) % 2
            du, dv = (1 - owner_core) * u + owner_core * v, (1 - owner_core) * v + owner_core * u
            owner = ((x + du) % 2) * 4 + ((y + dv) % 2) * 2 + owner_core
            columns = pl.ds(pl.multiple_of(owner * CHUNK, CHUNK), CHUNK)
            at[r * CHUNK : (r + 1) * CHUNK, :] = a_ref[:, columns].T
            dyt[r * CHUNK : (r + 1) * CHUNK, :] = dy_ref[:, columns].T
        if not inner:
            acc[...] = jnp.zeros_like(acc)

    @pl.when(j >= 3)
    def _():
        k = j - 3
        copy_second(k).wait()
        s, r = k % 4, k % 4
        total = stay[s, 0].astype(F32) + r_core[r, 0].astype(F32) + r_first[r, 0].astype(F32) + r_second[r].astype(F32)
        out_ref[...] = total.astype(BF16)

    @pl.when((j >= 2) & (j < units + 2))
    def _():
        k = j - 2
        copy_first(k).wait()
        s = k % 4
        second[k % 2] = (stay[s, 1].astype(F32) + r_core[s, 1].astype(F32) + r_first[s, 1].astype(F32)).astype(BF16)
        copy_second(k).start()

    @pl.when((j >= 1) & (j < units + 1))
    def _():
        k = j - 1
        copy_core(k).wait()
        s = k % 4
        first[k % 2] = (stay[s, 2:].astype(F32) + r_core[s, 2:].astype(F32)).astype(BF16)
        copy_first(k).start()

    def body(width):
        @pl.loop(0, TOKENS // ROWS)
        def _(i):
            rows = pl.ds(pl.multiple_of(i * ROWS, ROWS), ROWS)
            if inner:
                gate, up = gate_ref[rows, :width], up_ref[rows, :width]
            else:
                a = a_ref[rows, :]
                gate = dot(a, wg_ref[:, :width])
                up = dot(a, wu_ref[:, :width])
            by_act = dot_nt(dy_ref[rows, :], wd_ref[:width, :]).astype(BF16).astype(F32)
            sig = jax.nn.sigmoid(gate)
            silu = gate * sig
            act_s[rows, :width] = (silu * up).astype(BF16)
            du = (by_act * silu).astype(BF16)
            dg = (by_act * up * (sig + silu * (1.0 - sig))).astype(BF16)
            dg_s[rows, :width] = dg
            du_s[rows, :width] = du
            if not inner:
                acc[rows, :] += dot_nt(dg, wg_ref[:, :width]) + dot_nt(du, wu_ref[:, :width])

        def gradients(c, into):
            half = pl.ds(c * 4 * CHUNK, 4 * CHUNK)
            for which, (left, right) in enumerate(((at, dg_s), (at, du_s), (dyt, act_s))):
                term = dot(left[half, :], right[:, :width]).astype(BF16)
                into[:, which, :, :width] = term.reshape(4, CHUNK, width)

        gradients(1, go.at[j % 2])
        copy_core(j).start()
        gradients(0, stay.at[j % 4])

    by_width(j, units, last, body)

    if not inner:

        @pl.when(j == units)
        def _():
            da_ref[...] = acc[...].astype(BF16)


def backward(layer, first, size, inner, collective_id, a, dy, wd, left, right):
    units = pl.cdiv(size, BLOCK)
    last = size - (units - 1) * BLOCK
    start = first // BLOCK
    whole = lambda j: (0, 0)
    unit = lambda j: start + jnp.minimum(j, units - 1)
    in_specs = [once((TOKENS, D), whole), once((TOKENS, D), whole), pl.BlockSpec((None, BLOCK, D), lambda j: (layer, unit(j), 0))]
    if inner:
        in_specs += [pl.BlockSpec((TOKENS, BLOCK), lambda j: (0, unit(j)))] * 2
    else:
        in_specs += [pl.BlockSpec((None, D, BLOCK), lambda j: (layer, 0, unit(j)))] * 2
    out_specs = [pl.BlockSpec((3, CHUNK, BLOCK), lambda j: (0, 0, jnp.clip(j - 3, 0, units - 1)))]
    out_shape = [jax.ShapeDtypeStruct((3, CHUNK, size), BF16)]
    scratch = [
        pltpu.VMEM((D, TOKENS), BF16),
        pltpu.VMEM((D, TOKENS), BF16),
        pltpu.VMEM((TOKENS, BLOCK), BF16),
        pltpu.VMEM((TOKENS, BLOCK), BF16),
        pltpu.VMEM((TOKENS, BLOCK), BF16),
        pltpu.VMEM((4, 4, 3, CHUNK, BLOCK), BF16),
        pltpu.VMEM((2, 4, 3, CHUNK, BLOCK), BF16),
        pltpu.VMEM((2, 2, 3, CHUNK, BLOCK), BF16),
        pltpu.VMEM((2, 3, CHUNK, BLOCK), BF16),
        pltpu.VMEM((4, 4, 3, CHUNK, BLOCK), BF16),
        pltpu.VMEM((4, 2, 3, CHUNK, BLOCK), BF16),
        pltpu.VMEM((4, 3, CHUNK, BLOCK), BF16),
    ] + [pltpu.SemaphoreType.DMA((units,))] * 6
    if not inner:
        out_specs.append(once((TOKENS, D), whole))
        out_shape.append(jax.ShapeDtypeStruct((TOKENS, D), BF16))
        scratch.append(pltpu.VMEM((TOKENS, D), F32))
    return pl.pallas_call(
        functools.partial(backward_kernel, units, last, inner),
        grid=(units + 3,),
        in_specs=in_specs,
        out_specs=out_specs,
        out_shape=out_shape,
        scratch_shapes=scratch,
        compiler_params=pltpu.CompilerParams(vmem_limit_bytes=VMEM, collective_id=collective_id, has_side_effects=True),
        cost_estimate=pl.CostEstimate(flops=(8 if inner else 16) * TOKENS * D * size, bytes_accessed=40_000_000, transcendentals=TOKENS * size),
        name=f"backward{layer}_{first}",
    )(a, dy, wd, left, right)


WIDE = 640


def adamw_kernel(g_ref, *refs):
    ins, outs = refs[:9], refs[-9:]
    for which in range(3):
        g = g_ref[which].astype(F32)
        if which == 2:
            g = g.T
        w, m, v = (ins[3 * kind + which][...].astype(F32) for kind in range(3))
        m = 0.9 * m + 0.1 * g
        v = 0.95 * v + 0.05 * g * g
        step = m * lax.rsqrt(v + 1e-8) + 0.1 * w
        outs[which][...] = (w - 0.02 * step).astype(BF16)
        outs[3 + which][...] = m
        outs[6 + which][...] = v


def adamw(layer, first, size, g, arrays, so_far):
    start = first // WIDE
    row = pl.BlockSpec((None, CHUNK, WIDE), lambda k, i: (layer, k, start + i))
    column = pl.BlockSpec((None, WIDE, CHUNK), lambda k, i: (layer, start + i, k))
    nine = [row, row, column] * 3
    in_specs = [pl.BlockSpec((None, 3, CHUNK, WIDE), lambda k, i: (k, 0, 0, i))] + nine
    aliases = {}
    if so_far:
        in_specs += [pl.BlockSpec(memory_space=pl.ANY)] * 9
        aliases = {10 + i: i for i in range(9)}
    types = [BF16] * 3 + [F32] * 6
    elements = 3 * D * size
    return pl.pallas_call(
        adamw_kernel,
        grid=(8, size // WIDE),
        in_specs=in_specs,
        out_specs=nine,
        out_shape=[jax.ShapeDtypeStruct(a.shape, t) for a, t in zip(arrays, types)],
        input_output_aliases=aliases,
        compiler_params=pltpu.CompilerParams(vmem_limit_bytes=VMEM),
        cost_estimate=pl.CostEstimate(flops=40 * elements, bytes_accessed=22 * elements, transcendentals=elements),
        name=f"adamw{layer}_{first}",
    )(g, *arrays, *so_far)


PIECES = ((0, 1280), (1280, 1920))


def solution(mesh):
    def step(x, dy, *arrays):
        wg, wu, wd = arrays[:3]
        x, dy = x[0], dy[0]
        gate, up, a0, h1, a1 = forward(x, wg, wu, wd)
        g1, da = backward(1, 0, FF, False, 0, a1, dy, wd, wg, wu)
        gathered = [(1, 0, FF, lax.all_gather(g1, "dp"))]
        h, d = h1.astype(F32), da.astype(F32)
        scale = rms(h)
        dh = d * scale - h * (scale**3 / D) * jnp.sum(d * h, -1, keepdims=True)
        dh1 = (dy.astype(F32) + dh.astype(BF16).astype(F32)).astype(BF16)
        own = None
        for number, (first, size) in enumerate(PIECES):
            (own,) = backward(0, first, size, True, 1 + number, a0, dh1, wd, gate, up)
            gathered.append((0, first, size, lax.all_gather(own, "dp")))
        outs = ()
        for layer, first, size, g in gathered:
            outs = adamw(layer, first, size, g, arrays, outs)
        return tuple(outs)

    return jax.shard_map(
        step,
        mesh=mesh,
        in_specs=(P(("rep", "dp"), None, None),) * 2 + (P(None, None, None),) * 9,
        out_specs=(P("rep", None, None),) * 9,
        check_vma=False,
    )
```

time: 1010 us -> 699 us (0.69)
  Pallas kernels: 0 us -> 669 us
  waiting for transfers between devices: 450 us -> 0.11 us
  matrix products: 371 us -> 0 us
  other arithmetic: 151 us -> 12.5 us
  local copies, waits for them, and re-layouts: 13 us -> 0 us
    pallas_call x0 -> x7, Pallas kernels: none -> 669 us  [the longest x3 443 us: backward(): pl.pallas_call(functools.partial(backward_kernel, units, last, inner), gr...]
    psum x1 -> x0, waiting for transfers between devices: 450 us -> none  [step(): summed[number] = [lax.psum(by_w[name], 'dp') for name in NAMES]]
    dot_general x15 -> x0, matrix products: 371 us -> none  [the longest x5 134 us: layer(): gate = jnp.dot(a, w['w_gate'], preferred_element_type=jnp.float32)]
    convert_element_type x2 -> x1, other arithmetic: 141 us -> 7.33 us  [step(): dh1 = (dy.astype(F32) + dh.astype(BF16).astype(F32)).astype(BF16)]
    unnamed x18 -> x0, local copies, waits for them, and re-layouts: 13 us -> none
  transfers between devices with their start and end apart: 1 -> 3, of which waited for: 1 -> 0; matrix products, arithmetic and copies ran while one was open for 0% -> 2% of each run, Pallas kernels for 0% -> 47%
where the time goes in v1:
time: 699 us; the launch traced here: 696 us
  Pallas kernels  669 us (96%)
  between operations  14.3 us (2%)
  other arithmetic  12.5 us (2%)
    pallas_call x3, Pallas kernels, backward(): pl.pallas_call(functools.partial(backward_kernel, units, last, inner), gr...  443 us
    pallas_call x3, Pallas kernels, adamw(): pl.pallas_call(adamw_kernel, grid=(8, size // WIDE), in_specs=in_specs, o...  162 us
    pallas_call x1, Pallas kernels, forward(): pl.pallas_call(functools.partial(forward_kernel, units, last), grid=(unit...  64.2 us
  transfers between devices with their start and end apart: 3, of which 0 were waited for; matrix products, arithmetic and copies ran while one was open for 2% of the time, Pallas kernels for 47%

profile of v1, /device:TPU:0, one launch (start us, length us, event | category | flops | bytes accessed | tf_op | source)
XLA Modules:
  0.0 695.9 jit_solution(6310534682478167115)
XLA Ops:
  7.2 0.0 all-gather.11.cloned.1.call-start
  7.2 64.2 %forward0.1 = (f32[2048,3200]{1,0:T(8,128)}, f32[2048,3200]{1,0:T(8,128)}, bf16[2048,1024]{1,0:T(8,128)(2,1)}, bf16[2048,1024]{1,0:T(8,128)(2,1)}, bf16[2048,1024]{1,0:T(8,128)(2,1)}) custom-call(bf16[2048,1024]{1,0:T(8,128)(2,1)} %bitcast.10, bf16[2,1024,3200]{2,1,0:T(8,128)(2,1)} %refs_0_.5, bf16[2,1024,3200]{2,1,0:T(8,128)(2,1)} %refs_1_.5, ...), custom_call_target="tpu_custom_call" | custom-call | flops 40265318400 | bytes 90000000 | tf_op jit(solution)/shard_map/forward0/pallas_call | solution.py:85
  71.5 227.2 %backward1_0.1 = (bf16[3,128,3200]{2,1,0:T(8,128)(2,1)}, bf16[2048,1024]{1,0:T(8,128)(2,1)}) custom-call(bf16[2048,1024]{1,0:T(8,128)(2,1)} %get-tuple-element.35.refs_0_, bf16[2048,1024]{1,0:T(8,128)(2,1)} %bitcast.9, bf16[2,3200,1024]{2,1,0:T(8,128)(2,1)} %refs_2_.11, bf16[2,1024,3200]{2,1,0:T(8,128)(2,1)} %refs_0_.5, bf16[2,1024,3200]{2,1,0:T(8,128)(2,1)} %refs_1_.5), custom_call_target="tpu_custom_call" | custom-call | flops 107374182400 | bytes 40000000 | tf_op jit(solution)/shard_map/backward1_0/pallas_call | solution.py:255
  298.7 0.0 all-gather.11.cloned.1.call-update
  298.7 0.0 all-gather.9.cloned.1.call-start
  298.8 5.2 fusion.2
  304.0 7.3 %add_convert_fusion.refs_1_ = bf16[2048,1024]{1,0:T(8,128)(2,1)} fusion(bf16[2048,1024]{1,0:T(8,128)(2,1)} %get-tuple-element.37, bf16[2048,1024]{1,0:T(8,128)(2,1)} %get-tuple-element.36, f32[2048]{0:T(1024)S(1)} %get-tuple-element.60, f32[2048]{0:T(1024)S(1)} %get-tuple-element.62, f32[2048]{0:T(1024)S(1)} %get-tuple-element.61, ...), kind=kLoop, calls=%fused_computation.9 | loop fusion | flops 23068672 | bytes 16801792 | tf_op jit(solution)/shard_map/convert_element_type | solution.py:324
  311.3 103.5 %backward0_0.1 = bf16[3,128,1280]{2,1,0:T(8,128)(2,1)} custom-call(bf16[2048,1024]{1,0:T(8,128)(2,1)} %get-tuple-element.34.refs_0_, bf16[2048,1024]{1,0:T(8,128)(2,1)} %add_convert_fusion.refs_1_, bf16[2,3200,1024]{2,1,0:T(8,128)(2,1)} %refs_2_.11, f32[2048,3200]{1,0:T(8,128)} %get-tuple-element.38.refs_3_, f32[2048,3200]{1,0:T(8,128)} %get-tuple-element.39.refs_4_), custom_call_target="tpu_custom_call" | custom-call | flops 21474836480 | bytes 40000000 | tf_op jit(solution)/shard_map/backward0_0/pallas_call | solution.py:255
  414.9 0.0 all-gather.9.cloned.1.call-update
  414.9 0.0 all-gather.7.cloned.1.call-start
  414.9 111.8 %backward0_1280.1 = bf16[3,128,1920]{2,1,0:T(8,128)(2,1)} custom-call(bf16[2048,1024]{1,0:T(8,128)(2,1)} %get-tuple-element.34.refs_0_, bf16[2048,1024]{1,0:T(8,128)(2,1)} %add_convert_fusion.refs_1_, bf16[2,3200,1024]{2,1,0:T(8,128)(2,1)} %refs_2_.11, f32[2048,3200]{1,0:T(8,128)} %get-tuple-element.38.refs_3_, f32[2048,3200]{1,0:T(8,128)} %get-tuple-element.39.refs_4_), custom_call_target="tpu_custom_call" | custom-call | flops 32212254720 | bytes 40000000 | tf_op jit(solution)/shard_map/backward0_1280/pallas_call | solution.py:255
  526.7 0.0 all-gather.7.cloned.1.call-update
  526.8 0.0 all-gather.11.cloned.1.call-done
  526.8 80.7 %adamw1_0.1 = (bf16[2,1024,3200]{2,1,0:T(8,128)(2,1)}, bf16[2,1024,3200]{2,1,0:T(8,128)(2,1)}, bf16[2,3200,1024]{2,1,0:T(8,128)(2,1)}, f32[2,1024,3200]{2,1,0:T(...) custom-call(bf16[8,3,128,3200]{3,2,1,0:T(8,128)(2,1)} %bitcast.6, ...), custom_call_target="tpu_custom_call" | custom-call | flops 393216000 | bytes 216268800 | tf_op jit(solution)/shard_map/adamw1_0/pallas_call | solution.py:298
  607.5 0.0 all-gather.9.cloned.1.call-done
  607.5 32.7 %adamw0_0.1 = (bf16[2,1024,3200]{2,1,0:T(8,128)(2,1)}, bf16[2,1024,3200]{2,1,0:T(8,128)(2,1)}, bf16[2,3200,1024]{2,1,0:T(8,128)(2,1)}, f32[2,1024,3200]{2,1,0:T(...) custom-call(bf16[8,3,128,1280]{3,2,1,0:T(8,128)(2,1)} %bitcast.8, ...), custom_call_target="tpu_custom_call", output_to_operand_aliasing={{0}: (10, {}), {1}: (11, {}), {2}: (12, {}), {3}: (13, {}),... | custom-call | flops 157286400 | bytes 86507520 | tf_op jit(solution)/shard_map/adamw0_0/pallas_call | solution.py:298
  640.2 0.0 all-gather.7.cloned.1.call-done
  640.2 48.7 %adamw0_1280.1 = (bf16[2,1024,3200]{2,1,0:T(8,128)(2,1)}, bf16[2,1024,3200]{2,1,0:T(8,128)(2,1)}, bf16[2,3200,1024]{2,1,0:T(8,128)(2,1)}, f32[2,1024,3200]{2,1,0...) custom-call(bf16[8,3,128,1920]{3,2,1,0:T(8,128)(2,1)} %bitcast.7, ...), custom_call_target="tpu_custom_call", output_to_operand_aliasing={{0}: (10, {}), {1}: (11, {}), {2}: (12, {}), {3}: (13, {}),... | custom-call | flops 235929600 | bytes 129761280 | tf_op jit(solution)/shard_map/adamw0_1280/pallas_call | solution.py:298
  (1 shorter events, 0.0 us)
Async XLA Ops:
  7.2 519.6 %all-gather.11.cloned.1.call-start = ((), (), s32[]{:S(2)}) async-start(), calls=%async_computation.2 | async-start | bytes 22118400 | tf_op jit(solution)/shard_map/all_gather | solution.py:320
  298.7 308.8 %all-gather.9.cloned.1.call-start = ((), (), s32[]{:S(2)}) async-start(), calls=%async_computation.1 | async-start | bytes 8847360 | tf_op jit(solution)/shard_map/all_gather | solution.py:328
  414.9 225.3 %all-gather.7.cloned.1.call-start = ((), (), s32[]{:S(2)}) async-start(), calls=%async_computation | async-start | bytes 13271040 | tf_op jit(solution)/shard_map/all_gather | solution.py:328
Sparse Core Ops, SparseCore 0:
  298.8 124.5 all-gather.10
  425.3 64.7 all-gather.8
  526.9 62.8 all-gather.6

commit v2 on v1

--- a/solution.py
+++ b/solution.py
@@ -10,7 +10,10 @@
 NAMES = ("w_gate", "w_up", "w_down")
 TOKENS, D, FF = 2048, 1024, 3200
 BLOCK = 256
-ROWS = 512
+ROWS = 1024
+LAG = 2
+STEPS = 2 * LAG + 1
+SLOTS = STEPS + 1
 CHUNK = D // 8
 VMEM = 66_000_000
 NT = (((1,), (1,)), ((), ()))
@@ -46,17 +49,15 @@
 
     @pl.when(j == 0)
     def _():
-        @pl.loop(0, TOKENS // ROWS)
-        def _(i):
-            rows = pl.ds(pl.multiple_of(i * ROWS, ROWS), ROWS)
+        for i in range(TOKENS // ROWS):
+            rows = slice(i * ROWS, (i + 1) * ROWS)
             wide = x_ref[rows, :].astype(F32)
             a_ref[rows, :] = (wide * rms(wide)).astype(BF16)
             acc[rows, :] = jnp.zeros((ROWS, D), F32)
 
     def body(width):
-        @pl.loop(0, TOKENS // ROWS)
-        def _(i):
-            rows = pl.ds(pl.multiple_of(i * ROWS, ROWS), ROWS)
+        for i in range(TOKENS // ROWS):
+            rows = slice(i * ROWS, (i + 1) * ROWS)
             a = a_ref[rows, :]
             gate = dot(a, wg_ref[:, :width])
             up = dot(a, wu_ref[:, :width])
@@ -69,9 +70,8 @@
 
     @pl.when(j == units - 1)
     def _():
-        @pl.loop(0, TOKENS // ROWS)
-        def _(i):
-            rows = pl.ds(pl.multiple_of(i * ROWS, ROWS), ROWS)
+        for i in range(TOKENS // ROWS):
+            rows = slice(i * ROWS, (i + 1) * ROWS)
             h = (x_ref[rows, :].astype(F32) + acc[rows, :].astype(BF16).astype(F32)).astype(BF16)
             h_ref[rows, :] = h
             wide = h.astype(F32)
@@ -111,11 +111,10 @@
         a_ref, dy_ref, wd_ref, gate_ref, up_ref, out_ref = refs[:6]
         rest = refs[6:]
     else:
-        a_ref, dy_ref, wd_ref, wg_ref, wu_ref, out_ref, da_ref = refs[:7]
-        rest = refs[7:]
-    at, dyt, act_s, dg_s, du_s, stay, go, first, second, r_core, r_first, r_second = rest[:12]
-    sems = rest[12:18]
-    acc = None if inner else rest[18]
+        a_ref, dy_ref, wd_ref, wg_ref, wu_ref, out_ref, dg_out, du_out = refs[:8]
+        rest = refs[8:]
+    at, dyt, act_s, dgu_s, stay, go, first, second, r_core, r_first, r_second = rest[:11]
+    sems = rest[11:17]
     core_send, core_recv, first_send, first_recv, second_send, second_recv = sems
     j = pl.program_id(0)
     me = lax.axis_index("dp")
@@ -127,17 +126,17 @@
 
     def copy_core(k):
         return pltpu.make_async_remote_copy(
-            go.at[k % 2], r_core.at[k % 4], core_send.at[k], core_recv.at[k], device_id={"dp": partner}, device_id_type=pl.DeviceIdType.MESH
+            go.at[k % 2], r_core.at[k % SLOTS], core_send.at[k], core_recv.at[k], device_id={"dp": partner}, device_id_type=pl.DeviceIdType.MESH
         )
 
     def copy_first(k):
         return pltpu.make_async_remote_copy(
-            first.at[k % 2], r_first.at[k % 4], first_send.at[k], first_recv.at[k], device_id={"dp": one}, device_id_type=pl.DeviceIdType.MESH
+            first.at[k % 2], r_first.at[k % SLOTS], first_send.at[k], first_recv.at[k], device_id={"dp": one}, device_id_type=pl.DeviceIdType.MESH
         )
 
     def copy_second(k):
         return pltpu.make_async_remote_copy(
-            second.at[k % 2], r_second.at[k % 4], second_send.at[k], second_recv.at[k], device_id={"dp": two}, device_id_type=pl.DeviceIdType.MESH
+            second.at[k % 2], r_second.at[k % SLOTS], second_send.at[k], second_recv.at[k], device_id={"dp": two}, device_id_type=pl.DeviceIdType.MESH
         )
 
     @pl.when(j == 0)
@@ -154,22 +153,20 @@
             columns = pl.ds(pl.multiple_of(owner * CHUNK, CHUNK), CHUNK)
             at[r * CHUNK : (r + 1) * CHUNK, :] = a_ref[:, columns].T
             dyt[r * CHUNK : (r + 1) * CHUNK, :] = dy_ref[:, columns].T
-        if not inner:
-            acc[...] = jnp.zeros_like(acc)
-
-    @pl.when(j >= 3)
-    def _():
-        k = j - 3
+
+    @pl.when(j >= STEPS)
+    def _():
+        k = j - STEPS
         copy_second(k).wait()
-        s, r = k % 4, k % 4
-        total = stay[s, 0].astype(F32) + r_core[r, 0].astype(F32) + r_first[r, 0].astype(F32) + r_second[r].astype(F32)
+        s = k % SLOTS
+        total = stay[s, 0].astype(F32) + r_core[s, 0].astype(F32) + r_first[s, 0].astype(F32) + r_second[s].astype(F32)
         out_ref[...] = total.astype(BF16)
 
-    @pl.when((j >= 2) & (j < units + 2))
-    def _():
-        k = j - 2
+    @pl.when((j >= LAG + 1) & (j < units + LAG + 1))
+    def _():
+        k = j - LAG - 1
         copy_first(k).wait()
-        s = k % 4
+        s = k % SLOTS
         second[k % 2] = (stay[s, 1].astype(F32) + r_core[s, 1].astype(F32) + r_first[s, 1].astype(F32)).astype(BF16)
         copy_second(k).start()
 
@@ -177,14 +174,13 @@
     def _():
         k = j - 1
         copy_core(k).wait()
-        s = k % 4
+        s = k % SLOTS
         first[k % 2] = (stay[s, 2:].astype(F32) + r_core[s, 2:].astype(F32)).astype(BF16)
         copy_first(k).start()
 
     def body(width):
-        @pl.loop(0, TOKENS // ROWS)
-        def _(i):
-            rows = pl.ds(pl.multiple_of(i * ROWS, ROWS), ROWS)
+        for i in range(TOKENS // ROWS):
+            rows = slice(i * ROWS, (i + 1) * ROWS)
             if inner:
                 gate, up = gate_ref[rows, :width], up_ref[rows, :width]
             else:
@@ -197,28 +193,24 @@
             act_s[rows, :width] = (silu * up).astype(BF16)
             du = (by_act * silu).astype(BF16)
             dg = (by_act * up * (sig + silu * (1.0 - sig))).astype(BF16)
-            dg_s[rows, :width] = dg
-            du_s[rows, :width] = du
+            dgu_s[rows, :width] = dg
+            dgu_s[rows, width : 2 * width] = du
             if not inner:
-                acc[rows, :] += dot_nt(dg, wg_ref[:, :width]) + dot_nt(du, wu_ref[:, :width])
+                dg_out[rows, :width] = dg
+                du_out[rows, :width] = du
 
         def gradients(c, into):
             half = pl.ds(c * 4 * CHUNK, 4 * CHUNK)
-            for which, (left, right) in enumerate(((at, dg_s), (at, du_s), (dyt, act_s))):
-                term = dot(left[half, :], right[:, :width]).astype(BF16)
-                into[:, which, :, :width] = term.reshape(4, CHUNK, width)
+            term = dot(at[half, :], dgu_s[:, : 2 * width]).astype(BF16)
+            into[:, 0, :, :width] = term[:, :width].reshape(4, CHUNK, width)
+            into[:, 1, :, :width] = term[:, width:].reshape(4, CHUNK, width)
+            into[:, 2, :, :width] = dot(dyt[half, :], act_s[:, :width]).astype(BF16).reshape(4, CHUNK, width)
 
         gradients(1, go.at[j % 2])
         copy_core(j).start()
-        gradients(0, stay.at[j % 4])
+        gradients(0, stay.at[j % SLOTS])
 
     by_width(j, units, last, body)
-
-    if not inner:
-
-        @pl.when(j == units)
-        def _():
-            da_ref[...] = acc[...].astype(BF16)
 
 
 def backward(layer, first, size, inner, collective_id, a, dy, wd, left, right):
@@ -232,37 +224,64 @@
         in_specs += [pl.BlockSpec((TOKENS, BLOCK), lambda j: (0, unit(j)))] * 2
     else:
         in_specs += [pl.BlockSpec((None, D, BLOCK), lambda j: (layer, 0, unit(j)))] * 2
-    out_specs = [pl.BlockSpec((3, CHUNK, BLOCK), lambda j: (0, 0, jnp.clip(j - 3, 0, units - 1)))]
+    out_specs = [pl.BlockSpec((3, CHUNK, BLOCK), lambda j: (0, 0, jnp.clip(j - STEPS, 0, units - 1)))]
     out_shape = [jax.ShapeDtypeStruct((3, CHUNK, size), BF16)]
     scratch = [
         pltpu.VMEM((D, TOKENS), BF16),
         pltpu.VMEM((D, TOKENS), BF16),
         pltpu.VMEM((TOKENS, BLOCK), BF16),
-        pltpu.VMEM((TOKENS, BLOCK), BF16),
-        pltpu.VMEM((TOKENS, BLOCK), BF16),
-        pltpu.VMEM((4, 4, 3, CHUNK, BLOCK), BF16),
+        pltpu.VMEM((TOKENS, 2 * BLOCK), BF16),
+        pltpu.VMEM((SLOTS, 4, 3, CHUNK, BLOCK), BF16),
         pltpu.VMEM((2, 4, 3, CHUNK, BLOCK), BF16),
         pltpu.VMEM((2, 2, 3, CHUNK, BLOCK), BF16),
         pltpu.VMEM((2, 3, CHUNK, BLOCK), BF16),
-        pltpu.VMEM((4, 4, 3, CHUNK, BLOCK), BF16),
-        pltpu.VMEM((4, 2, 3, CHUNK, BLOCK), BF16),
-        pltpu.VMEM((4, 3, CHUNK, BLOCK), BF16),
+        pltpu.VMEM((SLOTS, 4, 3, CHUNK, BLOCK), BF16),
+        pltpu.VMEM((SLOTS, 2, 3, CHUNK, BLOCK), BF16),
+        pltpu.VMEM((SLOTS, 3, CHUNK, BLOCK), BF16),
     ] + [pltpu.SemaphoreType.DMA((units,))] * 6
     if not inner:
-        out_specs.append(once((TOKENS, D), whole))
-        out_shape.append(jax.ShapeDtypeStruct((TOKENS, D), BF16))
-        scratch.append(pltpu.VMEM((TOKENS, D), F32))
+        out_specs += [pl.BlockSpec((TOKENS, BLOCK), lambda j: (0, jnp.minimum(j, units - 1)))] * 2
+        out_shape += [jax.ShapeDtypeStruct((TOKENS, size), BF16)] * 2
     return pl.pallas_call(
         functools.partial(backward_kernel, units, last, inner),
-        grid=(units + 3,),
+        grid=(units + STEPS,),
         in_specs=in_specs,
         out_specs=out_specs,
         out_shape=out_shape,
         scratch_shapes=scratch,
         compiler_params=pltpu.CompilerParams(vmem_limit_bytes=VMEM, collective_id=collective_id, has_side_effects=True),
-        cost_estimate=pl.CostEstimate(flops=(8 if inner else 16) * TOKENS * D * size, bytes_accessed=40_000_000, transcendentals=TOKENS * size),
+        cost_estimate=pl.CostEstimate(flops=(8 if inner else 12) * TOKENS * D * size, bytes_accessed=40_000_000, transcendentals=TOKENS * size),
         name=f"backward{layer}_{first}",
     )(a, dy, wd, left, right)
+
+
+def input_kernel(pieces, *refs):
+    grads, (wg_ref, wu_ref, h_ref, dy_ref, out_ref) = refs[: 2 * len(pieces)], refs[2 * len(pieces) :]
+    da = None
+    for number, (first, size) in enumerate(pieces):
+        for g_ref, w_ref in zip(grads[2 * number : 2 * number + 2], (wg_ref, wu_ref)):
+            part = dot_nt(g_ref[...], w_ref[:, first : first + size])
+            da = part if da is None else da + part
+    h, d = h_ref[...].astype(F32), da.astype(BF16).astype(F32)
+    scale = rms(h)
+    dh = d * scale - h * (scale**3 / D) * jnp.sum(d * h, -1, keepdims=True)
+    out_ref[...] = (dy_ref[...].astype(F32) + dh.astype(BF16).astype(F32)).astype(BF16)
+
+
+def by_input(layer, pieces, grads, wg, wu, h, dy):
+    rows = 256
+    weight = once((None, D, FF), lambda i: (layer, 0, 0))
+    state = pl.BlockSpec((rows, D), lambda i: (i, 0))
+    return pl.pallas_call(
+        functools.partial(input_kernel, pieces),
+        grid=(TOKENS // rows,),
+        in_specs=[pl.BlockSpec((rows, size), lambda i: (i, 0)) for _, size in pieces for _ in range(2)] + [weight, weight, state, state],
+        out_specs=state,
+        out_shape=jax.ShapeDtypeStruct((TOKENS, D), BF16),
+        compiler_params=pltpu.CompilerParams(vmem_limit_bytes=VMEM),
+        cost_estimate=pl.CostEstimate(flops=4 * TOKENS * D * FF, bytes_accessed=50_000_000, transcendentals=TOKENS),
+        name="by_input",
+    )(*grads, wg, wu, h, dy)
 
 
 WIDE = 640
@@ -308,7 +327,7 @@
     )(g, *arrays, *so_far)
 
 
-PIECES = ((0, 1280), (1280, 1920))
+PIECES = ((0, 1920), (1920, 1280))
 
 
 def solution(mesh):
@@ -316,16 +335,11 @@
         wg, wu, wd = arrays[:3]
         x, dy = x[0], dy[0]
         gate, up, a0, h1, a1 = forward(x, wg, wu, wd)
-        g1, da = backward(1, 0, FF, False, 0, a1, dy, wd, wg, wu)
-        gathered = [(1, 0, FF, lax.all_gather(g1, "dp"))]
-        h, d = h1.astype(F32), da.astype(F32)
-        scale = rms(h)
-        dh = d * scale - h * (scale**3 / D) * jnp.sum(d * h, -1, keepdims=True)
-        dh1 = (dy.astype(F32) + dh.astype(BF16).astype(F32)).astype(BF16)
-        own = None
-        for number, (first, size) in enumerate(PIECES):
-            (own,) = backward(0, first, size, True, 1 + number, a0, dh1, wd, gate, up)
-            gathered.append((0, first, size, lax.all_gather(own, "dp")))
+        own, *grads = backward(1, 0, FF, False, 0, a1, dy, wd, wg, wu)
+        gathered = [(1, 0, FF, lax.all_gather(own, "dp"))]
+        dh1 = by_input(1, ((0, FF),), grads, wg, wu, h1, dy)
+        (own,) = backward(0, 0, FF, True, 1, a0, dh1, wd, gate, up)
+        gathered += [(0, first, size, lax.all_gather(own[:, :, first : first + size], "dp")) for first, size in PIECES]
         outs = ()
         for layer, first, size, g in gathered:
             outs = adamw(layer, first, size, g, arrays, outs)

time: 699 us -> 562 us (0.80)
  Pallas kernels: 669 us -> 535 us
  other arithmetic: 12.5 us -> 0 us
    pallas_call x3 -> x2, Pallas kernels: 443 us -> 276 us  [backward(): pl.pallas_call(functools.partial(backward_kernel, units, last, inner), gr...]
    pallas_call x0 -> x1, Pallas kernels: none -> 39.5 us  [by_input(): pl.pallas_call(functools.partial(input_kernel, pieces), grid=(TOKENS // r...]
    convert_element_type x1 -> x0, other arithmetic: 7.33 us -> none  [step(): dh1 = (dy.astype(F32) + dh.astype(BF16).astype(F32)).astype(BF16)]
    pallas_call x1, Pallas kernels: 64.2 us -> 57.2 us  [forward(): pl.pallas_call(functools.partial(forward_kernel, units, last), grid=(unit...]
  transfers between devices with their start and end apart: 3 -> 3, of which waited for: 0 -> 0; matrix products, arithmetic and copies ran while one was open for 2% -> 1% of each run, Pallas kernels for 47% -> 56%
where the time goes in v2:
time: 562 us; the launch traced here: 554 us
  Pallas kernels  535 us (95%)
  between operations  14.3 us (3%)
    pallas_call x2, Pallas kernels, backward(): pl.pallas_call(functools.partial(backward_kernel, units, last, inner), gr...  276 us
    pallas_call x3, Pallas kernels, adamw(): pl.pallas_call(adamw_kernel, grid=(8, size // WIDE), in_specs=in_specs, o...  162 us
    pallas_call x1, Pallas kernels, forward(): pl.pallas_call(functools.partial(forward_kernel, units, last), grid=(unit...  57.2 us
    pallas_call x1, Pallas kernels, by_input(): pl.pallas_call(functools.partial(input_kernel, pieces), grid=(TOKENS // r...  39.5 us
  transfers between devices with their start and end apart: 3, of which 0 were waited for; matrix products, arithmetic and copies ran while one was open for 1% of the time, Pallas kernels for 56%

profile of v2, /device:TPU:0, one launch (start us, length us, event | category | flops | bytes accessed | tf_op | source)
XLA Modules:
  0.0 554.3 jit_solution(14432236064136891345)
XLA Ops:
  7.2 0.0 all-gather.11.cloned.1.call-start
  7.2 57.2 %forward0.1 = (f32[2048,3200]{1,0:T(8,128)}, f32[2048,3200]{1,0:T(8,128)}, bf16[2048,1024]{1,0:T(8,128)(2,1)}, bf16[2048,1024]{1,0:T(8,128)(2,1)}, bf16[2048,1024]{1,0:T(8,128)(2,1)}) custom-call(bf16[2048,1024]{1,0:T(8,128)(2,1)} %bitcast.8, bf16[2,1024,3200]{2,1,0:T(8,128)(2,1)} %refs_0_.5, bf16[2,1024,3200]{2,1,0:T(8,128)(2,1)} %refs_1_.5, ...), custom_call_target="tpu_custom_call" | custom-call | flops 40265318400 | bytes 90000000 | tf_op jit(solution)/shard_map/forward0/pallas_call | solution.py:85
  64.5 135.1 %backward1_0.1 = (bf16[3,128,3200]{2,1,0:T(8,128)(2,1)}, bf16[2048,3200]{1,0:T(8,128)(2,1)}, bf16[2048,3200]{1,0:T(8,128)(2,1)}) custom-call(bf16[2048,1024]{1,0:T(8,128)(2,1)} %get-tuple-element.36.refs_0_, bf16[2048,1024]{1,0:T(8,128)(2,1)} %bitcast.9, bf16[2,3200,1024]{2,1,0:T(8,128)(2,1)} %refs_2_.11, bf16[2,1024,3200]{2,1,0:T(8,128)(2,1)} %refs_0_.5, ...), custom_call_target="tpu_custom_call" | custom-call | flops 80530636800 | bytes 40000000 | tf_op jit(solution)/shard_map/backward1_0/pallas_call | solution.py:245
  199.5 0.0 all-gather.11.cloned.1.call-update
  199.6 0.0 all-gather.9.cloned.1.call-start
  199.6 39.5 %by_input.1.refs_1_ = bf16[2048,1024]{1,0:T(8,128)(2,1)} custom-call(bf16[2048,3200]{1,0:T(8,128)(2,1)} %get-tuple-element.37.refs_0_, bf16[2048,3200]{1,0:T(8,128)(2,1)} %get-tuple-element.38.refs_1_, bf16[2,1024,3200]{2,1,0:T(8,128)(2,1)} %refs_0_.5, bf16[2,1024,3200]{2,1,0:T(8,128)(2,1)} %refs_1_.5, bf16[2048,1024]{1,0:T(8,128)(2,1)} %get-tuple-element.39.refs_4_, ...), custom_call_target="tpu_custom_call" | custom-call | flops 26843545600 | bytes 50000000 | tf_op jit(solution)/shard_map/by_input/pallas_call | solution.py:275
  239.1 140.9 %backward0_0.1 = bf16[3,128,3200]{2,1,0:T(8,128)(2,1)} custom-call(bf16[2048,1024]{1,0:T(8,128)(2,1)} %get-tuple-element.35.refs_0_, bf16[2048,1024]{1,0:T(8,128)(2,1)} %by_input.1.refs_1_, bf16[2,3200,1024]{2,1,0:T(8,128)(2,1)} %refs_2_.11, f32[2048,3200]{1,0:T(8,128)} %get-tuple-element.40.refs_3_, f32[2048,3200]{1,0:T(8,128)} %get-tuple-element.41.refs_4_), custom_call_target="tpu_custom_call" | custom-call | flops 53687091200 | bytes 40000000 | tf_op jit(solution)/shard_map/backward0_0/pallas_call | solution.py:245
  380.0 2.6 slice.7
  382.6 0.0 all-gather.9.cloned.1.call-update
  382.6 0.0 all-gather.7.cloned.1.call-start
  382.7 2.2 slice.6
  384.9 0.0 all-gather.7.cloned.1.call-update
  384.9 0.0 all-gather.11.cloned.1.call-done
  385.0 80.9 %adamw1_0.1 = (bf16[2,1024,3200]{2,1,0:T(8,128)(2,1)}, bf16[2,1024,3200]{2,1,0:T(8,128)(2,1)}, bf16[2,3200,1024]{2,1,0:T(8,128)(2,1)}, f32[2,1024,3200]{2,1,0:T(...) custom-call(bf16[8,3,128,3200]{3,2,1,0:T(8,128)(2,1)} %bitcast.5, ...), custom_call_target="tpu_custom_call" | custom-call | flops 393216000 | bytes 216268800 | tf_op jit(solution)/shard_map/adamw1_0/pallas_call | solution.py:317
  465.9 0.0 all-gather.9.cloned.1.call-done
  465.9 48.7 %adamw0_0.1 = (bf16[2,1024,3200]{2,1,0:T(8,128)(2,1)}, bf16[2,1024,3200]{2,1,0:T(8,128)(2,1)}, bf16[2,3200,1024]{2,1,0:T(8,128)(2,1)}, f32[2,1024,3200]{2,1,0:T(...) custom-call(bf16[8,3,128,1920]{3,2,1,0:T(8,128)(2,1)} %bitcast.6, ...), custom_call_target="tpu_custom_call", output_to_operand_aliasing={{0}: (10, {}), {1}: (11, {}), {2}: (12, {}), {3}: (13, {}),... | custom-call | flops 235929600 | bytes 129761280 | tf_op jit(solution)/shard_map/adamw0_0/pallas_call | solution.py:317
  514.6 0.0 all-gather.7.cloned.1.call-done
  514.6 32.7 %adamw0_1920.1 = (bf16[2,1024,3200]{2,1,0:T(8,128)(2,1)}, bf16[2,1024,3200]{2,1,0:T(8,128)(2,1)}, bf16[2,3200,1024]{2,1,0:T(8,128)(2,1)}, f32[2,1024,3200]{2,1,0...) custom-call(bf16[8,3,128,1280]{3,2,1,0:T(8,128)(2,1)} %bitcast.7, ...), custom_call_target="tpu_custom_call", output_to_operand_aliasing={{0}: (10, {}), {1}: (11, {}), {2}: (12, {}), {3}: (13, {}),... | custom-call | flops 157286400 | bytes 86507520 | tf_op jit(solution)/shard_map/adamw0_1920/pallas_call | solution.py:317
Async XLA Ops:
  7.2 377.8 %all-gather.11.cloned.1.call-start = ((), (), s32[]{:S(2)}) async-start(), calls=%async_computation.2 | async-start | bytes 22118400 | tf_op jit(solution)/shard_map/all_gather | solution.py:339
  199.6 266.4 %all-gather.9.cloned.1.call-start = ((), (), s32[]{:S(2)}) async-start(), calls=%async_computation.1 | async-start | bytes 13271040 | tf_op jit(solution)/shard_map/all_gather | solution.py:342
  382.6 132.0 %all-gather.7.cloned.1.call-start = ((), (), s32[]{:S(2)}) async-start(), calls=%async_computation | async-start | bytes 8847360 | tf_op jit(solution)/shard_map/all_gather | solution.py:342
Sparse Core Ops, SparseCore 0:
  199.7 122.6 all-gather.10
  382.7 62.7 all-gather.8
  447.4 46.1 all-gather.6
